TPU v7x, 128 devices: a whole 4x4x4 slice. The times are simulated.
128 devices in a mesh: task: 8 (over x_hi, y), tp: 16 (over z, x_lo, core).
Axes of the slice: x: 4 (x_hi: 2, x_lo: 2; x = x_hi * 2 + x_lo), y: 4, z: 4, core: 2. Of those that a mesh axis runs over, the one named last changes fastest.
Arguments:
- observations: bfloat16 [256, 16, 4096], P('task', None, 'tp'), may hold values from -6 to 6
- gain: float32 [4096], P('tp'), may hold values from 0.5 to 1.5
- w_in: bfloat16 [4096, 4096], P(None, 'tp'), may hold values from -0.09375 to 0.09375
- w_mix: bfloat16 [4096, 4096], P('tp'), may hold values from -0.09375 to 0.09375
- w_out: bfloat16 [4096, 4096], P(None, 'tp'), may hold values from -0.09375 to 0.09375
- w_head: bfloat16 [4096, 75], P('tp'), may hold values from -0.09375 to 0.09375
- head_bias: float32 [75], replicated, may hold values from -4 to 4
- pop_mean: float32 [57], replicated, may hold values from -8 to 8
- pop_scale: float32 [57], replicated, may hold values from 0.5 to 4
- task_indices: int32 [256], P('task'), may hold values from 0 to 56
- actions: int32 [256, 15], P('task'), may hold values from 0 to 17
- rewards: float32 [256, 15], P('task'), may hold values from -18 to 27
- episode_ends: int32 [256, 15], P('task'), may hold values 0 or 1
- behaviour_log_prob: float32 [256, 15], P('task'), may hold values from -4.5 to -1.5
Outputs:
- grad_w_in: float32 [4096, 4096], P(None, 'tp')
- grad_w_mix: float32 [4096, 4096], P('tp')
- grad_w_out: float32 [4096, 4096], P(None, 'tp')
- grad_gain: float32 [4096], P('tp')
- grad_head: float32 [4096, 75], P('tp')
- grad_head_bias: float32 [75], replicated
- new_head: bfloat16 [4096, 75], P('tp')
- new_bias: float32 [75], replicated
- updated_return_mean: float32 [57], replicated
- updated_return_scale: float32 [57], replicated
All inputs are finite; a program needn't handle non-finite values. No bound on the sum of `episode_ends` on one device may be relied on, other than what follows from the above.
Results may differ from a plain program's by a relative error of at most 0.03.
Values may be sent and summed in bfloat16 or wider, within the bound.
A program may use at most 128 MiB of HBM per device.

v0:
```python
import jax
import jax.numpy as jnp
from jax import lax
from jax.sharding import PartitionSpec as P

ACTIONS = 18
TASKS = 57
DISCOUNT = 0.99
BASELINE_COST = 0.5
ENTROPY_COST = 0.01
POPART_PRIOR = 64.0
NORM_EPS = 1e-06


def sent_to_all(value, axis):
    copies = jnp.broadcast_to(value, (lax.axis_size(axis), *value.shape))
    return lax.all_to_all(copies, axis, split_axis=0, concat_axis=0, tiled=True)


def of_everyone(value, axis):
    everything = sent_to_all(value, axis)
    return jnp.sum(everything, axis=0)


def packed_total(arrays, axis):
    line, at, gathered = (jnp.concatenate([a.reshape(-1) for a in arrays]), 0, [])
    subtotal = of_everyone(line, axis)
    for a in arrays:
        gathered.append(subtotal[at : at + a.size].reshape(a.shape))
        at += a.size
    return tuple(gathered)


def cut_along(value, dim, devices):
    before, after = (value.shape[:dim], value.shape[dim + 1 :])
    return jnp.moveaxis(value.reshape(*before, devices, -1, *after), dim, 0)


def sum_at_owner(value, axis, dim):
    parts = cut_along(value, dim, lax.axis_size(axis))
    arrived = lax.all_to_all(parts, axis, split_axis=0, concat_axis=0, tiled=True)
    return arrived.astype(jnp.float32).sum(axis=0)


def joined_along(parts, dim):
    dims = list(parts.shape[1:])
    dims[dim] *= parts.shape[0]
    return jnp.moveaxis(parts, 0, dim).reshape(dims)


def gathered_copies(value, axis, dim):
    parts = sent_to_all(value, axis)
    return joined_along(parts, dim)


def summed_on_arrival(value, axis, dim):
    parts = cut_along(value, dim, lax.axis_size(axis))
    arrived = lax.all_to_all(parts, axis, split_axis=0, concat_axis=0, tiled=True)
    return arrived.sum(axis=0)


def silu_slope(before):
    sigmoid = jax.nn.sigmoid(before)
    return sigmoid * (1.0 + before * (1.0 - sigmoid))


def discounted_sums(values, factors):

    def advance(running, column):
        latest = column[0] + column[1] * running
        return (latest, latest)

    opening = jnp.zeros((values.shape[0],), jnp.float32)
    ending, stacked = lax.scan(advance, opening, (values.T, factors.T), reverse=True)
    return stacked.T


def task_onehot(task_indices):
    return (task_indices[:, None] == jnp.arange(TASKS, dtype=jnp.int32)[None, :]).astype(
        jnp.float32
    )


def popart_partials(task_indices, rewards, discount_factors):
    returns = discounted_sums(rewards, discount_factors)
    task_table = task_onehot(task_indices)
    counts = jnp.sum(task_table, axis=0) * rewards.shape[1]
    totals = jnp.dot(task_table.T, jnp.sum(returns, axis=1))
    squares = jnp.dot(task_table.T, jnp.sum(returns * returns, axis=1))
    return (counts, totals, squares)


def popart_update(counts, totals, squares, pop_mean, pop_scale):
    mixing = counts / (counts + POPART_PRIOR)
    safe_counts = jnp.maximum(counts, 1.0)
    batch_mean = totals / safe_counts
    batch_square = squares / safe_counts
    updated_return_mean = (1.0 - mixing) * pop_mean + mixing * batch_mean
    mean_gap = batch_mean - pop_mean
    variance = (
        (1.0 - mixing) * pop_scale * pop_scale
        + mixing * (batch_square - batch_mean * batch_mean)
        + mixing * (1.0 - mixing) * mean_gap * mean_gap
    )
    return (updated_return_mean, jnp.sqrt(variance))


def rescale_head(w_head, head_bias, pop_mean, pop_scale, updated_return_mean, updated_return_scale):
    scale_ratio = pop_scale / updated_return_scale
    column_scale = jnp.concatenate([jnp.ones((ACTIONS,), jnp.float32), scale_ratio])
    new_head = (w_head.astype(jnp.float32) * column_scale[None, :]).astype(jnp.bfloat16)
    value_bias = (
        pop_scale * head_bias[ACTIONS:] + pop_mean - updated_return_mean
    ) / updated_return_scale
    new_bias = jnp.concatenate([head_bias[:ACTIONS], value_bias])
    return (new_head, new_bias)


def importance_trace_loss(
    head_value_estimates,
    task_indices,
    actions,
    rewards,
    discount_factors,
    behaviour_log_prob,
    updated_return_mean,
    updated_return_scale,
    loss_weighting,
):
    task_table = task_onehot(task_indices)
    env_mean = jnp.dot(task_table, updated_return_mean)[:, None]
    env_scale = jnp.dot(task_table, updated_return_scale)[:, None]
    logits = head_value_estimates[:, :-1, :ACTIONS]
    norm_values = jnp.sum(head_value_estimates[:, :, ACTIONS:] * task_table[:, None, :], axis=2)
    values = lax.stop_gradient(norm_values * env_scale + env_mean)
    log_total = jnp.log(jnp.sum(jnp.exp(logits), axis=2))
    chosen = actions[:, :, None] == jnp.arange(ACTIONS, dtype=jnp.int32)[None, None, :]
    log_policy = jnp.sum(jnp.where(chosen, logits, 0.0), axis=2) - log_total
    clipped = jnp.minimum(jnp.exp(lax.stop_gradient(log_policy) - behaviour_log_prob), 1.0)
    deltas = clipped * (rewards + discount_factors * values[:, 1:] - values[:, :-1])
    targets = values[:, :-1] + discounted_sums(deltas, discount_factors * clipped)
    following = jnp.concatenate([targets[:, 1:], values[:, -1:]], axis=1)
    advantage = lax.stop_gradient(
        clipped
        * ((rewards + discount_factors * following - env_mean) / env_scale - norm_values[:, :-1])
    )
    normed_targets = lax.stop_gradient((targets - env_mean) / env_scale)
    policy = jnp.exp(logits - log_total[:, :, None])
    entropy = -jnp.sum(policy * (logits - log_total[:, :, None]), axis=2)
    per_frame = (
        -advantage * log_policy
        + 0.5 * BASELINE_COST * (normed_targets - norm_values[:, :-1]) ** 2
        - ENTROPY_COST * entropy
    )
    return loss_weighting * jnp.sum(per_frame)


def on_device(
    observations,
    gain,
    w_in,
    w_mix,
    w_out,
    w_head,
    head_bias,
    pop_mean,
    pop_scale,
    task_indices,
    actions,
    rewards,
    episode_ends,
    behaviour_log_prob,
):
    env_count, frames, part_width = observations.shape
    groups = lax.axis_size("tp")
    full_width = part_width * groups
    row_count = env_count * frames
    local_rows = row_count // groups
    own_tokens = observations.reshape(row_count, part_width)
    discount_factors = DISCOUNT * (1.0 - episode_ends.astype(jnp.float32))
    counts, totals, squares = popart_partials(task_indices, rewards, discount_factors)
    counts, totals, squares = packed_total((counts, totals, squares), "task")
    updated_return_mean, updated_return_scale = popart_update(
        counts, totals, squares, pop_mean, pop_scale
    )
    new_head, new_bias = rescale_head(
        w_head, head_bias, pop_mean, pop_scale, updated_return_mean, updated_return_scale
    )
    loss_weighting = float(env_count * lax.axis_size("task")) ** (-0.5)
    tokens, gain_all = (
        lax.all_gather(own_tokens, "tp", axis=1, tiled=True),
        lax.all_gather(gain.astype(jnp.bfloat16), "tp", axis=0, tiled=True).astype(gain.dtype),
    )
    row_offset = lax.axis_index("tp") * local_rows
    token_rows = lax.dynamic_slice_in_dim(tokens, row_offset, local_rows, 0)
    pre_in = jnp.dot(tokens, w_in, preferred_element_type=jnp.float32)
    hidden_in = jax.nn.silu(pre_in).astype(jnp.bfloat16)
    hidden_rows = hidden_in
    mix_sum = lax.psum_scatter(
        jnp.dot(hidden_rows, w_mix, preferred_element_type=jnp.float32).astype(jnp.bfloat16),
        "tp",
        scatter_dimension=0,
        tiled=True,
    ).astype(jnp.float32)
    residual = token_rows.astype(jnp.float32) + mix_sum
    inverse = lax.rsqrt(jnp.mean(residual * residual, axis=1, keepdims=True) + NORM_EPS)
    normed = (residual * inverse * gain_all[None, :]).astype(jnp.bfloat16)
    normed_all = lax.all_gather(normed, "tp", axis=0, tiled=True)
    pre_out = jnp.dot(normed_all, w_out, preferred_element_type=jnp.float32)
    hidden_out = jax.nn.silu(pre_out).astype(jnp.bfloat16)
    head_terms = jnp.dot(hidden_out, new_head, preferred_element_type=jnp.float32)
    env_share = env_count // groups
    env_offset = lax.axis_index("tp") * env_share

    def select_envs(source):
        return lax.dynamic_slice_in_dim(source, env_offset, env_share, 0)

    head_value_estimates = (
        sum_at_owner(head_terms.astype(jnp.bfloat16), "tp", 0) + new_bias[None, :]
    )
    head_value_estimates = head_value_estimates.reshape(env_share, frames, -1)

    def share_loss(network_outputs):
        return importance_trace_loss(
            network_outputs,
            select_envs(task_indices),
            select_envs(actions),
            select_envs(rewards),
            select_envs(discount_factors),
            select_envs(behaviour_log_prob),
            updated_return_mean,
            updated_return_scale,
            loss_weighting,
        )

    loss_value, pullback = jax.vjp(share_loss, head_value_estimates)
    (d_heads,) = pullback(jnp.ones((), jnp.float32))
    d_local = d_heads.reshape(env_share * frames, -1).astype(jnp.bfloat16)
    d_rounded = gathered_copies(d_local, "tp", 0)
    grad_head = jnp.dot(hidden_out.T, d_rounded, preferred_element_type=jnp.float32)
    grad_bias = jnp.sum(d_rounded.astype(jnp.float32), axis=0)
    d_hidden_out = jnp.dot(d_rounded, new_head.T, preferred_element_type=jnp.float32)
    d_pre_out = (d_hidden_out * silu_slope(pre_out)).astype(jnp.bfloat16)
    grad_out = jnp.dot(normed_all.T, d_pre_out, preferred_element_type=jnp.float32)
    d_normed = lax.psum_scatter(
        jnp.dot(d_pre_out, w_out.T, preferred_element_type=jnp.float32).astype(jnp.bfloat16),
        "tp",
        scatter_dimension=0,
        tiled=True,
    ).astype(jnp.float32)
    scaled = d_normed * gain_all[None, :]
    inner_sum = jnp.sum(scaled * residual, axis=1, keepdims=True)
    d_residual = (inverse * scaled - residual * inverse**3 * inner_sum / full_width).astype(
        jnp.bfloat16
    )
    grad_gain = summed_on_arrival(jnp.sum(d_normed * residual * inverse, axis=0), "tp", 0)
    arrived = lax.all_gather(d_residual, "tp", axis=0, tiled=True)
    hidden_rows = hidden_in
    grad_part = jnp.dot(hidden_rows.T, arrived, preferred_element_type=jnp.float32)
    d_hidden = jnp.dot(arrived, w_mix.T, preferred_element_type=jnp.float32)
    grad_mix = grad_part
    d_pre_in = (d_hidden * silu_slope(pre_in)).astype(jnp.bfloat16)
    grad_in = jnp.dot(tokens.T, d_pre_in, preferred_element_type=jnp.float32)
    grad_in, grad_mix, grad_out, grad_gain, grad_head, grad_bias = (
        lax.psum(grad_in.astype(jnp.bfloat16), "task").astype(jnp.float32),
        lax.psum(grad_mix.astype(jnp.bfloat16), "task").astype(jnp.float32),
        lax.psum(grad_out.astype(jnp.bfloat16), "task").astype(jnp.float32),
        lax.psum(grad_gain.astype(jnp.bfloat16), "task").astype(jnp.float32),
        lax.psum(grad_head.astype(jnp.bfloat16), "task").astype(jnp.float32),
        lax.psum(grad_bias.astype(jnp.bfloat16), "task").astype(jnp.float32),
    )
    return (
        grad_in,
        grad_mix,
        grad_out,
        grad_gain,
        grad_head,
        grad_bias,
        new_head,
        new_bias,
        updated_return_mean,
        updated_return_scale,
    )


def solution(mesh):
    in_specs = (
        P("task", None, "tp"),
        P("tp"),
        P(None, "tp"),
        P("tp", None),
        P(None, "tp"),
        P("tp", None),
        P(),
        P(),
        P(),
        P("task"),
        P("task", None),
        P("task", None),
        P("task", None),
        P("task", None),
    )
    out_specs = (
        P(None, "tp"),
        P("tp", None),
        P(None, "tp"),
        P("tp"),
        P("tp", None),
        P(),
        P("tp", None),
        P(),
        P(),
        P(),
    )
    return jax.shard_map(
        on_device, mesh=mesh, in_specs=in_specs, out_specs=out_specs, check_vma=False
    )
```

profile of v0, /device:TPU:1, one launch (start us, length us, event | category | flops | bytes accessed | tf_op | source)
XLA Modules:
  0.0 498.5 jit_solution(18199204609391938755)
XLA Ops:
  7.2 0.7 all-gather.5.cloned.1.call-update
  8.0 50.4 %all-gather.5.cloned.1.call-done = bf16[512,4096]{1,0:T(8,128)(2,1)} async-done(((bf16[512,256]{1,0:T(8,128)(2,1)}), bf16[512,4096]{1,0:T(8,128)(2,1)}) %all-gather.5.cloned.1.call-update) | async-done | bytes 4194320 | tf_op jit(solution)/shard_map/all_gather | solution.py:191
  58.4 4.1 fusion.46
  62.5 3.3 convolution_convert_fusion.1
  66.0 18.6 %all-gather = bf16[16,1,256]{2,1,0:T(2,128)(2,1)S(1)} all-gather(bf16[1,1,256]{2,1,0:T(2,128)(2,1)S(1)} %reshape.98), channel_id=1, replica_groups=mesh['task'=8,'tp'=16] {'tp'}, dimensions={0}, use_global_device_ids=true | all-gather | bytes 8704 | tf_op jit(solution)/shard_map/all_gather | solution.py:192
  84.6 49.5 %reduce-scatter.3.cloned.1.call-done = bf16[32,4096]{1,0:T(8,128)(2,1)} async-done(((bf16[512,4096]{1,0:T(8,128)(2,1)}), bf16[32,4096]{1,0:T(8,128)(2,1)}) %reduce-scatter.3.cloned.1.call-update) | async-done | bytes 262160 | tf_op jit(solution)/shard_map/reduce_scatter | solution.py:199
  134.1 1.2 multiply_reduce_fusion
  135.3 0.5 multiply_multiply_fusion.1
  135.8 1.8 multiply_convert_fusion.1
  137.9 1.1 while.34
  139.1 0.1 convolution_bitcast_fusion.3
  139.2 0.1 convolution_bitcast_fusion.2
  139.5 0.6 broadcast_in_dim.72
  140.1 6.2 %all-to-all-start = ((f32[8,1,171]{2,1,0:T(1,128)}), f32[8,1,171]{2,1,0:T(1,128)S(1)}, u32[]{:S(2)}, u32[]{:S(2)}) async-start(f32[8,1,171]{2,1,0:T(1,128)} %broadcast_in_dim.72), calls=%async_computation.1 | async-start | bytes 16384 | tf_op jit(solution)/shard_map/all_to_all | solution.py:17
  146.9 6.0 %all-to-all-done = f32[8,1,171]{2,1,0:T(1,128)S(1)} async-done(((f32[8,1,171]{2,1,0:T(1,128)}), f32[8,1,171]{2,1,0:T(1,128)S(1)}, u32[]{:S(2)}, u32[]{:S(2)}) %all-to-all-start) | async-done | bytes 5504 | tf_op jit(solution)/shard_map/all_to_all | solution.py:17
  153.1 0.2 convolution_bitcast_fusion.1
  153.3 0.2 convolution_bitcast_fusion
  153.6 23.3 %all-gather.7.cloned.1.call-done = bf16[512,4096]{1,0:T(8,128)(2,1)} async-done(((bf16[32,4096]{1,0:T(8,128)(2,1)}), bf16[512,4096]{1,0:T(8,128)(2,1)}) %all-gather.7.cloned.1.call-update) | async-done | bytes 4194320 | tf_op jit(solution)/shard_map/all_gather | solution.py:208
  176.8 4.9 multiply_convert_fusion
  181.8 0.2 convolution_convert_fusion.5
  182.0 0.8 copy.88
  182.8 4.2 all-to-all-start.1
  187.0 6.0 %all-to-all-done.1 = bf16[16,32,75]{2,1,0:T(8,128)(2,1)S(1)} async-done(((bf16[16,32,75]{2,1,0:T(8,128)(2,1)}), bf16[16,32,75]{2,1,0:T(8,128)(2,1)S(1)}, u32[]{:S(2)}, u32[]{:S(2)}) %all-to-all-start.1) | async-done | bytes 76832 | tf_op jit(solution)/shard_map/all_to_all | solution.py:41
  193.2 0.2 fusion.19
  193.5 0.2 multiply_reduce_fusion.1
  194.0 1.1 while.35
  195.7 9.4 %all_to_all.25 = bf16[16,32,75]{2,1,0:T(8,128)(2,1)S(1)} all-to-all(bf16[16,32,75]{2,1,0:T(8,128)(2,1)S(1)} %broadcast_in_dim.79), channel_id=1, replica_groups=mesh['task'=8,'tp'=16] {'tp'}, dimensions={0} | all-to-all | bytes 153600 | tf_op jit(solution)/shard_map/all_to_all | solution.py:17
  205.1 1.3 fusion.5
  206.4 3.3 convolution_convert_fusion
  209.8 67.0 %reduce-scatter.5.cloned.1.call-done = bf16[32,4096]{1,0:T(8,128)(2,1)} async-done(((bf16[512,4096]{1,0:T(8,128)(2,1)}), bf16[32,4096]{1,0:T(8,128)(2,1)}) %reduce-scatter.5.cloned.1.call-update) | async-done | bytes 262160 | tf_op jit(solution)/shard_map/reduce_scatter | solution.py:245
  276.8 1.8 fusion.13
  278.7 2.0 fusion.10
  280.6 0.2 all-reduce.8.cloned.1.call-start
  280.9 4.8 convolution_convert_fusion.2
  285.7 33.9 %all-gather.9.cloned.1.call-done = bf16[512,4096]{1,0:T(8,128)(2,1)} async-done(((bf16[32,4096]{1,0:T(8,128)(2,1)}), bf16[512,4096]{1,0:T(8,128)(2,1)}) %all-gather.9.cloned.1.call-update) | async-done | bytes 4194320 | tf_op jit(solution)/shard_map/all_gather | solution.py:257
  319.6 9.4 %fusion.4 = bf16[4096,256]{0,1:T(8,128)(2,1)} fusion(bf16[512,4096]{1,0:T(8,128)(2,1)} %all-gather.5.cloned.1.call-done, bf16[512,4096]{1,0:T(8,128)(2,1)} %all-gather.9.cloned.1.call-done, bf16[256,4096]{1,0:T(8,128)(2,1)S(1)} %copy-done, f32[512,256]{1,0:T(8,128)S(1)} %fusion.46), kind=kOutput, calls=%fused_computation.11 | convolution fusion | flops 2149711872 | bytes 13107200 | tf_op jit(solution)/shard_map/dot_general | solution.py:263
  329.0 4.8 convolution_convert_fusion.3
  333.8 4.4 all-to-all-start.3
  338.2 0.2 convolution_convert_fusion.6
  338.5 5.5 %all-to-all-done.3 = f32[16,1,256]{2,1,0:T(1,128)S(1)} async-done(((f32[16,1,256]{2,1,0:T(1,128)}), f32[16,1,256]{2,1,0:T(1,128)S(1)}, u32[]{:S(2)}, u32[]{:S(2)}) %all-to-all-start.3) | async-done | bytes 16416 | tf_op jit(solution)/shard_map/all_to_all | solution.py:58
  344.0 38.7 %all-reduce.4 = (bf16[256]{0:T(256)(128)(2,1)S(1)}, bf16[256,75]{0,1:T(8,128)(2,1)S(1)}, bf16[75]{0:T(256)(128)(2,1)S(1)}) all-reduce(bf16[256]{0:T(256)(128)(2,1)S(1)} %reduce_sum.162, bf16[256,75]{0,1:T(8,128)(2,1)S(1)} %convolution_convert_fusion.6, bf16[75]{0:T(256)(128)(2,1)S(1)} %reduce_sum.163), channel_id=1, replica_groups=mesh['task'=8,'tp'=16] {'task'}, use_global_device_ids=true, to_apply=%region_23.24 | all-reduce | flops 19531 | bytes 78124 | tf_op jit(solution)/shard_map/psum | solution.py:268
  382.7 0.6 convert_element_type.138
  383.3 0.5 convert_element_type.141
  383.8 0.6 convert_element_type.140
  384.4 96.4 %all-reduce.8.cloned.1.call-done = (bf16[4096,256]{0,1:T(8,128)(2,1)}, bf16[256,4096]{1,0:T(8,128)(2,1)}, bf16[4096,256]{1,0:T(8,128)(2,1)}) async-done(((bf16[4096,256]{0,1:T(8,128)(2,1)}, bf16[256,4096]{1,0:T(8,128)(2,1)}, bf16[4096,256]{1,0:T(8,128)(2,1)}), (bf16[4096,256]{0,1:T(8,128)(2,1)}, bf16[256,4096]{1,0:T(8,128)(2,1)}, bf16[4096,256]{1,0:T(8,128)(2,1)})) %all-reduce.8.cloned.1.call-update) | async-done | bytes 6291472 | tf_op jit(solution)/shard_map/psum | solution.py:265
  480.8 4.3 copy.105
  485.1 4.2 convert_element_type.134
  489.3 2.3 convert_element_type.136
  (156 shorter events, 4.7 us)
Async XLA Ops:
  7.2 55.3 %copy-start = (bf16[256,4096]{1,0:T(8,128)(2,1)S(1)}, bf16[256,4096]{1,0:T(8,128)(2,1)}, u32[]{:S(2)}) copy-start(bf16[256,4096]{1,0:T(8,128)(2,1)} %param.21) | copy-start | bytes 6291460
  7.2 51.2 %all-gather.5.cloned.1.call-start = ((), (), s32[]{:S(2)}) async-start(), calls=%async_computation.6 | async-start | bytes 4456448 | tf_op jit(solution)/shard_map/all_gather | solution.py:191
  7.9 126.2 %reduce-scatter.3.cloned.1.call-start = ((), (), s32[]{:S(2)}) async-start(), calls=%async_computation.7 | async-start | bytes 4456448 | tf_op jit(solution)/shard_map/reduce_scatter | solution.py:199
  62.5 3.5 copy-start.17
  65.8 71.9 %copy-start.7 = (s32[32,15]{0,1:T(8,128)S(1)}, s32[32,15]{0,1:T(8,128)}, u32[]{:S(2)}) copy-start(s32[32,15]{0,1:T(8,128)} %param.30) | copy-start | bytes 5764
  65.8 72.1 %copy-start.6 = (f32[32,15]{0,1:T(8,128)S(1)}, f32[32,15]{0,1:T(8,128)}, u32[]{:S(2)}) copy-start(f32[32,15]{0,1:T(8,128)} %param.29) | copy-start | bytes 5764
  65.8 73.3 %copy-start.18 = (s32[32]{0:T(128)S(1)}, s32[32]{0:T(128)}, u32[]{:S(2)}) copy-start(s32[32]{0:T(128)} %param.27) | copy-start | bytes 388
  65.8 80.6 %copy-start.9 = (f32[32,15]{0,1:T(8,128)S(1)}, f32[32,15]{0,1:T(8,128)}, u32[]{:S(2)}) copy-start(f32[32,15]{0,1:T(8,128)} %param.31) | copy-start | bytes 5764
  65.8 80.7 %copy-start.8 = (s32[32,15]{0,1:T(8,128)S(1)}, s32[32,15]{0,1:T(8,128)}, u32[]{:S(2)}) copy-start(s32[32,15]{0,1:T(8,128)} %param.28) | copy-start | bytes 5764
  65.8 87.1 %copy-start.12 = (f32[57]{0:T(128)S(1)}, f32[57]{0:T(128)}, u32[]{:S(2)}) copy-start(f32[57]{0:T(128)} %param.25) | copy-start | bytes 688
  65.8 87.1 %copy-start.13 = (f32[57]{0:T(128)S(1)}, f32[57]{0:T(128)}, u32[]{:S(2)}) copy-start(f32[57]{0:T(128)} %param.26) | copy-start | bytes 688
  65.8 87.0 %copy-start.14 = (f32[75]{0:T(128)S(1)}, f32[75]{0:T(128)}, u32[]{:S(2)}) copy-start(f32[75]{0:T(128)} %param.24) | copy-start | bytes 904
  65.9 87.6 %copy-start.5 = (bf16[256,75]{0,1:T(8,128)(2,1)S(1)}, bf16[256,75]{0,1:T(8,128)(2,1)}, u32[]{:S(2)}) copy-start(bf16[256,75]{0,1:T(8,128)(2,1)} %param.23) | copy-start | bytes 115204
  65.9 111.0 %all-gather.7.cloned.1.call-start = ((), (), s32[]{:S(2)}) async-start(), calls=%async_computation.8 | async-start | bytes 4456448 | tf_op jit(solution)/shard_map/all_gather | solution.py:208
  135.8 1.9 copy-start.10
  140.1 12.7 %all-to-all-start = ((f32[8,1,171]{2,1,0:T(1,128)}), f32[8,1,171]{2,1,0:T(1,128)S(1)}, u32[]{:S(2)}, u32[]{:S(2)}) async-start(f32[8,1,171]{2,1,0:T(1,128)} %broadcast_in_dim.72), calls=%async_computation.1 | async-start | bytes 16384 | tf_op jit(solution)/shard_map/all_to_all | solution.py:17
  153.0 28.8 %copy-start.15 = (f32[57]{0:T(128)}, f32[57]{0:T(128)S(1)}, u32[]{:S(2)}) copy-start(f32[57]{0:T(128)S(1)} %get-tuple-element.394) | copy-start | bytes 688
  153.0 28.8 %copy-start.16 = (f32[57]{0:T(128)}, f32[57]{0:T(128)S(1)}, u32[]{:S(2)}) copy-start(f32[57]{0:T(128)S(1)} %get-tuple-element.395) | copy-start | bytes 688
  153.6 51.5 %copy-start.4 = (bf16[256,75]{0,1:T(8,128)(2,1)}, bf16[256,75]{0,1:T(8,128)(2,1)S(1)}, u32[]{:S(2)}) copy-start(bf16[256,75]{0,1:T(8,128)(2,1)S(1)} %multiply_convert_fusion.3) | copy-start | bytes 115204
  182.8 10.3 %all-to-all-start.1 = ((bf16[16,32,75]{2,1,0:T(8,128)(2,1)}), bf16[16,32,75]{2,1,0:T(8,128)(2,1)S(1)}, u32[]{:S(2)}, u32[]{:S(2)}) async-start(bf16[16,32,75]{2,1,0:T(8,128)(2,1)} %bitcast.8), calls=%async_computation.2 | async-start | bytes 262144 | tf_op jit(solution)/shard_map/all_to_all | solution.py:41
  186.9 89.9 %reduce-scatter.5.cloned.1.call-start = ((), (), s32[]{:S(2)}) async-start(), calls=%async_computation.9 | async-start | bytes 4456448 | tf_op jit(solution)/shard_map/reduce_scatter | solution.py:245
  187.0 6.0 %copy-start.11 = (f32[75]{0:T(128)}, f32[75]{0:T(128)S(1)}, u32[]{:S(2)}) copy-start(f32[75]{0:T(128)S(1)} %pad_maximum_fusion.1) | copy-start | bytes 904
  195.2 11.2 %copy-start.3 = (bf16[4096,256]{1,0:T(8,128)(2,1)S(1)}, bf16[4096,256]{1,0:T(8,128)(2,1)}, u32[]{:S(2)}) copy-start(bf16[4096,256]{1,0:T(8,128)(2,1)} %param.22) | copy-start | bytes 6291460
  209.7 67.1 %copy-start.1 = (bf16[32,4096]{1,0:T(8,128)(2,1)S(1)}, bf16[32,4096]{1,0:T(8,128)(2,1)}, u32[]{:S(2)}) copy-start(bf16[32,4096]{1,0:T(8,128)(2,1)} %reduce-scatter.3.cloned.1.call-done) | copy-start | bytes 786436
  209.7 109.8 %all-gather.9.cloned.1.call-start = ((), (), s32[]{:S(2)}) async-start(), calls=%async_computation.10 | async-start | bytes 4456448 | tf_op jit(solution)/shard_map/all_gather | solution.py:257
  280.6 200.2 %all-reduce.8.cloned.1.call-start = ((), (), s32[]{:S(2)}) async-start(), calls=%async_computation.11 | async-start | bytes 12582912 | tf_op jit(solution)/shard_map/psum | solution.py:265
  333.8 10.1 %all-to-all-start.3 = ((f32[16,1,256]{2,1,0:T(1,128)}), f32[16,1,256]{2,1,0:T(1,128)S(1)}, u32[]{:S(2)}, u32[]{:S(2)}) async-start(f32[16,1,256]{2,1,0:T(1,128)} %bitcast.20), calls=%async_computation.5 | async-start | bytes 32768 | tf_op jit(solution)/shard_map/all_to_all | solution.py:58
  485.1 4.3 copy-start.2
Sparse Core Ops, SparseCore 0:
  9.6 48.6 all-gather.4
  66.0 68.0 reduce-scatter.2
  137.8 38.9 all-gather.6
  209.9 66.9 reduce-scatter.4
  280.8 38.7 all-gather.8
  333.9 146.8 all-reduce.7
where the time goes:
time: 499 us
  waiting for transfers between devices  339 us (68%)
  blocking collectives  66.7 us (13%)
  matrix products  37 us (7%)
  other arithmetic  18 us (4%)
  starting transfers between devices  15.1 us (3%)
  between operations  14.4 us (3%)
  local copies, waits for them, and re-layouts  8.14 us (2%)
    psum x1, waiting for transfers between devices, on_device(): lax.psum(grad_in.astype(jnp.bfloat16), 'task').astype(jnp.float32)  96.4 us
    reduce_scatter x1, waiting for transfers between devices, on_device(): lax.psum_scatter(jnp.dot(d_pre_out, w_out.T, preferred_element_type=jnp.f...  67 us
    all_gather x1, waiting for transfers between devices, on_device(): lax.all_gather(own_tokens, 'tp', axis=1, tiled=True)  50.4 us
    reduce_scatter x1, waiting for transfers between devices, on_device(): lax.psum_scatter(jnp.dot(hidden_rows, w_mix, preferred_element_type=jnp.f...  49.5 us
    psum x1, blocking collectives, on_device(): lax.psum(grad_gain.astype(jnp.bfloat16), 'task').astype(jnp.float32)  38.7 us
    all_gather x1, waiting for transfers between devices, on_device(): arrived = lax.all_gather(d_residual, 'tp', axis=0, tiled=True)  33.9 us
    all_gather x1, waiting for transfers between devices, on_device(): normed_all = lax.all_gather(normed, 'tp', axis=0, tiled=True)  23.3 us
    all_gather x1, blocking collectives, on_device(): lax.all_gather(gain.astype(jnp.bfloat16), 'tp', axis=0, tiled=True)  18.6 us
  transfers between devices with their start and end apart: 9, of which 9 were waited for; matrix products, arithmetic and copies ran while one was open for 2% of the time, Pallas kernels for 0%

commit v1 on v0

--- a/solution.py
+++ b/solution.py
@@ -10,6 +10,13 @@
 ENTROPY_COST = 0.01
 POPART_PRIOR = 64.0
 NORM_EPS = 1e-06
+
+
+def all_by_exchange(x, mesh_axis, dim):
+    devices = lax.axis_size(mesh_axis)
+    tiles = jnp.stack([x for _ in range(devices)])
+    tiles = lax.all_to_all(tiles, mesh_axis, split_axis=0, concat_axis=0)
+    return jnp.concatenate(tiles, axis=dim)
 
 
 def sent_to_all(value, axis):
@@ -254,7 +261,7 @@
         jnp.bfloat16
     )
     grad_gain = summed_on_arrival(jnp.sum(d_normed * residual * inverse, axis=0), "tp", 0)
-    arrived = lax.all_gather(d_residual, "tp", axis=0, tiled=True)
+    arrived = all_by_exchange(d_residual, "tp", 0)
     hidden_rows = hidden_in
     grad_part = jnp.dot(hidden_rows.T, arrived, preferred_element_type=jnp.float32)
     d_hidden = jnp.dot(arrived, w_mix.T, preferred_element_type=jnp.float32)

time: 499 us -> 519 us (1.040)
  waiting for transfers between devices: 339 us -> 350 us
  starting transfers between devices: 15.1 us -> 22.1 us
    all_to_all x0 -> x1, waiting for transfers between devices: none -> 44.6 us  [all_by_exchange(): tiles = lax.all_to_all(tiles, mesh_axis, split_axis=0, concat_axis=0)]
    all_gather x1 -> x0, waiting for transfers between devices: 33.9 us -> none  [on_device(): arrived = lax.all_gather(d_residual, 'tp', axis=0, tiled=True)]
    all_to_all x0 -> x1, starting transfers between devices: none -> 7.16 us  [all_by_exchange(): tiles = lax.all_to_all(tiles, mesh_axis, split_axis=0, concat_axis=0)]
where the time goes in v1:
time: 519 us; the launch traced here: 518 us
  waiting for transfers between devices  350 us (67%)
  blocking collectives  66.7 us (13%)
  matrix products  37 us (7%)
  starting transfers between devices  22.1 us (4%)
  other arithmetic  17.3 us (3%)
  between operations  14.1 us (3%)
  local copies, waits for them, and re-layouts  10.7 us (2%)
    psum x1, waiting for transfers between devices, on_device(): lax.psum(grad_in.astype(jnp.bfloat16), 'task').astype(jnp.float32)  96.7 us
    reduce_scatter x1, waiting for transfers between devices, on_device(): lax.psum_scatter(jnp.dot(d_pre_out, w_out.T, preferred_element_type=jnp.f...  67.1 us
    all_gather x1, waiting for transfers between devices, on_device(): lax.all_gather(own_tokens, 'tp', axis=1, tiled=True)  50.4 us
    reduce_scatter x1, waiting for transfers between devices, on_device(): lax.psum_scatter(jnp.dot(hidden_rows, w_mix, preferred_element_type=jnp.f...  49.5 us
    all_to_all x1, waiting for transfers between devices, all_by_exchange(): tiles = lax.all_to_all(tiles, mesh_axis, split_axis=0, concat_axis=0)  44.6 us
    psum x1, blocking collectives, on_device(): lax.psum(grad_gain.astype(jnp.bfloat16), 'task').astype(jnp.float32)  38.7 us
    all_gather x1, waiting for transfers between devices, on_device(): normed_all = lax.all_gather(normed, 'tp', axis=0, tiled=True)  23.3 us
    all_gather x1, blocking collectives, on_device(): lax.all_gather(gain.astype(jnp.bfloat16), 'tp', axis=0, tiled=True)  18.6 us
  transfers between devices with their start and end apart: 9, of which 9 were waited for; matrix products, arithmetic and copies ran while one was open for 2% of the time, Pallas kernels for 0%

profile of v1, /device:TPU:1, one launch (start us, length us, event | category | flops | bytes accessed | tf_op | source)
XLA Modules:
  0.0 518.1 jit_solution(10609982780571305390)
XLA Ops:
  7.2 0.7 all-gather.4.cloned.1.call-update
  8.0 50.4 %all-gather.4.cloned.1.call-done = bf16[512,4096]{1,0:T(8,128)(2,1)} async-done(((bf16[512,256]{1,0:T(8,128)(2,1)}), bf16[512,4096]{1,0:T(8,128)(2,1)}) %all-gather.4.cloned.1.call-update) | async-done | bytes 4194320 | tf_op jit(solution)/shard_map/all_gather | solution.py:198
  58.4 4.1 fusion.46
  62.5 3.3 convolution_convert_fusion.1
  66.0 18.6 %all-gather = bf16[16,1,256]{2,1,0:T(2,128)(2,1)S(1)} all-gather(bf16[1,1,256]{2,1,0:T(2,128)(2,1)S(1)} %reshape.104), channel_id=1, replica_groups=mesh['task'=8,'tp'=16] {'tp'}, dimensions={0}, use_global_device_ids=true | all-gather | bytes 8704 | tf_op jit(solution)/shard_map/all_gather | solution.py:199
  84.6 49.5 %reduce-scatter.3.cloned.1.call-done = bf16[32,4096]{1,0:T(8,128)(2,1)} async-done(((bf16[512,4096]{1,0:T(8,128)(2,1)}), bf16[32,4096]{1,0:T(8,128)(2,1)}) %reduce-scatter.3.cloned.1.call-update) | async-done | bytes 262160 | tf_op jit(solution)/shard_map/reduce_scatter | solution.py:206
  134.1 1.2 multiply_reduce_fusion
  135.3 0.5 multiply_multiply_fusion.1
  135.8 1.8 multiply_convert_fusion.1
  137.9 1.1 while.34
  139.5 0.6 broadcast_in_dim.72
  140.1 6.2 %all-to-all-start = ((f32[8,1,171]{2,1,0:T(1,128)}), f32[8,1,171]{2,1,0:T(1,128)S(1)}, u32[]{:S(2)}, u32[]{:S(2)}) async-start(f32[8,1,171]{2,1,0:T(1,128)} %broadcast_in_dim.72), calls=%async_computation.1 | async-start | bytes 16384 | tf_op jit(solution)/shard_map/all_to_all | solution.py:24
  146.9 6.0 %all-to-all-done = f32[8,1,171]{2,1,0:T(1,128)S(1)} async-done(((f32[8,1,171]{2,1,0:T(1,128)}), f32[8,1,171]{2,1,0:T(1,128)S(1)}, u32[]{:S(2)}, u32[]{:S(2)}) %all-to-all-start) | async-done | bytes 5504 | tf_op jit(solution)/shard_map/all_to_all | solution.py:24
  153.1 0.2 convolution_bitcast_fusion.1
  153.3 0.2 convolution_bitcast_fusion
  153.6 23.3 %all-gather.6.cloned.1.call-done = bf16[512,4096]{1,0:T(8,128)(2,1)} async-done(((bf16[32,4096]{1,0:T(8,128)(2,1)}), bf16[512,4096]{1,0:T(8,128)(2,1)}) %all-gather.6.cloned.1.call-update) | async-done | bytes 4194320 | tf_op jit(solution)/shard_map/all_gather | solution.py:215
  176.8 4.9 multiply_convert_fusion
  181.8 0.2 convolution_convert_fusion.5
  182.0 0.8 copy.88
  182.8 4.2 all-to-all-start.1
  187.0 6.0 %all-to-all-done.1 = bf16[16,32,75]{2,1,0:T(8,128)(2,1)S(1)} async-done(((bf16[16,32,75]{2,1,0:T(8,128)(2,1)}), bf16[16,32,75]{2,1,0:T(8,128)(2,1)S(1)}, u32[]{:S(2)}, u32[]{:S(2)}) %all-to-all-start.1) | async-done | bytes 76832 | tf_op jit(solution)/shard_map/all_to_all | solution.py:48
  193.2 0.2 fusion.19
  193.5 0.2 multiply_reduce_fusion.1
  194.0 1.1 while.35
  195.7 9.4 %all_to_all.30 = bf16[16,32,75]{2,1,0:T(8,128)(2,1)S(1)} all-to-all(bf16[16,32,75]{2,1,0:T(8,128)(2,1)S(1)} %broadcast_in_dim.79), channel_id=1, replica_groups=mesh['task'=8,'tp'=16] {'tp'}, dimensions={0} | all-to-all | bytes 153600 | tf_op jit(solution)/shard_map/all_to_all | solution.py:24
  205.1 1.3 fusion.5
  206.4 3.3 convolution_convert_fusion
  209.7 67.1 %reduce-scatter.5.cloned.1.call-done = bf16[32,4096]{1,0:T(8,128)(2,1)} async-done(((bf16[512,4096]{1,0:T(8,128)(2,1)}), bf16[32,4096]{1,0:T(8,128)(2,1)}) %reduce-scatter.5.cloned.1.call-update) | async-done | bytes 262160 | tf_op jit(solution)/shard_map/reduce_scatter | solution.py:252
  276.8 1.8 fusion.13
  278.7 1.3 fusion.10
  279.9 2.5 stack.2
  282.4 7.2 %all-to-all-start.3 = ((bf16[16,32,4096]{2,1,0:T(8,128)(2,1)}), bf16[16,32,4096]{2,1,0:T(8,128)(2,1)}, u32[]{:S(2)}, u32[]{:S(2)}) async-start(bf16[16,32,4096]{2,1,0:T(8,128)(2,1)} %stack.2), calls=%async_computation.5 | async-start | bytes 8388608 | tf_op jit(solution)/shard_map/all_to_all | solution.py:18
  289.6 0.2 all-reduce.8.cloned.1.call-start
  289.8 4.8 convolution_convert_fusion.2
  294.7 44.6 %all-to-all-done.3 = bf16[16,32,4096]{2,1,0:T(8,128)(2,1)} async-done(((bf16[16,32,4096]{2,1,0:T(8,128)(2,1)}), bf16[16,32,4096]{2,1,0:T(8,128)(2,1)}, u32[]{:S(2)}, u32[]{:S(2)}) %all-to-all-start.3) | async-done | bytes 4194336 | tf_op jit(solution)/shard_map/all_to_all | solution.py:18
  339.2 4.8 convolution_convert_fusion.3
  344.0 9.4 %fusion.4 = bf16[4096,256]{0,1:T(8,128)(2,1)} fusion(bf16[512,4096]{1,0:T(8,128)(2,1)} %all-gather.4.cloned.1.call-done, bf16[512,4096]{1,0:T(8,128)(2,1)} %bitcast.19, bf16[256,4096]{1,0:T(8,128)(2,1)S(1)} %copy-done, f32[512,256]{1,0:T(8,128)S(1)} %fusion.46), kind=kOutput, calls=%fused_computation.11 | convolution fusion | flops 2149711872 | bytes 13107200 | tf_op jit(solution)/shard_map/dot_general | solution.py:270
  353.5 4.3 all-to-all-start.4
  357.7 0.2 convolution_convert_fusion.6
  358.0 5.5 %all-to-all-done.4 = f32[16,1,256]{2,1,0:T(1,128)S(1)} async-done(((f32[16,1,256]{2,1,0:T(1,128)}), f32[16,1,256]{2,1,0:T(1,128)S(1)}, u32[]{:S(2)}, u32[]{:S(2)}) %all-to-all-start.4) | async-done | bytes 16416 | tf_op jit(solution)/shard_map/all_to_all | solution.py:65
  363.6 38.7 %all-reduce.4 = (bf16[256]{0:T(256)(128)(2,1)S(1)}, bf16[256,75]{0,1:T(8,128)(2,1)S(1)}, bf16[75]{0:T(256)(128)(2,1)S(1)}) all-reduce(bf16[256]{0:T(256)(128)(2,1)S(1)} %reduce_sum.162, bf16[256,75]{0,1:T(8,128)(2,1)S(1)} %convolution_convert_fusion.6, bf16[75]{0:T(256)(128)(2,1)S(1)} %reduce_sum.163), channel_id=1, replica_groups=mesh['task'=8,'tp'=16] {'task'}, use_global_device_ids=true, to_apply=%region_23.24 | all-reduce | flops 19531 | bytes 78124 | tf_op jit(solution)/shard_map/psum | solution.py:275
  402.3 0.6 convert_element_type.138
  402.8 0.5 convert_element_type.141
  403.4 0.6 convert_element_type.140
  404.0 96.7 %all-reduce.8.cloned.1.call-done = (bf16[4096,256]{0,1:T(8,128)(2,1)}, bf16[256,4096]{1,0:T(8,128)(2,1)}, bf16[4096,256]{1,0:T(8,128)(2,1)}) async-done(((bf16[4096,256]{0,1:T(8,128)(2,1)}, bf16[256,4096]{1,0:T(8,128)(2,1)}, bf16[4096,256]{1,0:T(8,128)(2,1)}), (bf16[4096,256]{0,1:T(8,128)(2,1)}, bf16[256,4096]{1,0:T(8,128)(2,1)}, bf16[4096,256]{1,0:T(8,128)(2,1)})) %all-reduce.8.cloned.1.call-update) | async-done | bytes 6291472 | tf_op jit(solution)/shard_map/psum | solution.py:272
  500.7 4.3 copy.105
  505.0 4.2 convert_element_type.134
  509.2 2.3 convert_element_type.136
  (156 shorter events, 4.9 us)
Async XLA Ops:
  7.2 55.3 %copy-start = (bf16[256,4096]{1,0:T(8,128)(2,1)S(1)}, bf16[256,4096]{1,0:T(8,128)(2,1)}, u32[]{:S(2)}) copy-start(bf16[256,4096]{1,0:T(8,128)(2,1)} %param.21) | copy-start | bytes 6291460
  7.2 51.2 %all-gather.4.cloned.1.call-start = ((), (), s32[]{:S(2)}) async-start(), calls=%async_computation.7 | async-start | bytes 4456448 | tf_op jit(solution)/shard_map/all_gather | solution.py:198
  7.9 126.2 %reduce-scatter.3.cloned.1.call-start = ((), (), s32[]{:S(2)}) async-start(), calls=%async_computation.8 | async-start | bytes 4456448 | tf_op jit(solution)/shard_map/reduce_scatter | solution.py:206
  62.5 3.5 copy-start.17
  65.8 71.9 %copy-start.7 = (s32[32,15]{0,1:T(8,128)S(1)}, s32[32,15]{0,1:T(8,128)}, u32[]{:S(2)}) copy-start(s32[32,15]{0,1:T(8,128)} %param.30) | copy-start | bytes 5764
  65.8 72.1 %copy-start.6 = (f32[32,15]{0,1:T(8,128)S(1)}, f32[32,15]{0,1:T(8,128)}, u32[]{:S(2)}) copy-start(f32[32,15]{0,1:T(8,128)} %param.29) | copy-start | bytes 5764
  65.8 73.3 %copy-start.18 = (s32[32]{0:T(128)S(1)}, s32[32]{0:T(128)}, u32[]{:S(2)}) copy-start(s32[32]{0:T(128)} %param.27) | copy-start | bytes 388
  65.8 80.6 %copy-start.9 = (f32[32,15]{0,1:T(8,128)S(1)}, f32[32,15]{0,1:T(8,128)}, u32[]{:S(2)}) copy-start(f32[32,15]{0,1:T(8,128)} %param.31) | copy-start | bytes 5764
  65.8 80.7 %copy-start.8 = (s32[32,15]{0,1:T(8,128)S(1)}, s32[32,15]{0,1:T(8,128)}, u32[]{:S(2)}) copy-start(s32[32,15]{0,1:T(8,128)} %param.28) | copy-start | bytes 5764
  65.8 87.1 %copy-start.12 = (f32[57]{0:T(128)S(1)}, f32[57]{0:T(128)}, u32[]{:S(2)}) copy-start(f32[57]{0:T(128)} %param.25) | copy-start | bytes 688
  65.8 87.1 %copy-start.13 = (f32[57]{0:T(128)S(1)}, f32[57]{0:T(128)}, u32[]{:S(2)}) copy-start(f32[57]{0:T(128)} %param.26) | copy-start | bytes 688
  65.8 87.0 %copy-start.14 = (f32[75]{0:T(128)S(1)}, f32[75]{0:T(128)}, u32[]{:S(2)}) copy-start(f32[75]{0:T(128)} %param.24) | copy-start | bytes 904
  65.9 87.6 %copy-start.5 = (bf16[256,75]{0,1:T(8,128)(2,1)S(1)}, bf16[256,75]{0,1:T(8,128)(2,1)}, u32[]{:S(2)}) copy-start(bf16[256,75]{0,1:T(8,128)(2,1)} %param.23) | copy-start | bytes 115204
  65.9 111.0 %all-gather.6.cloned.1.call-start = ((), (), s32[]{:S(2)}) async-start(), calls=%async_computation.9 | async-start | bytes 4456448 | tf_op jit(solution)/shard_map/all_gather | solution.py:215
  135.8 1.9 copy-start.10
  140.1 12.7 %all-to-all-start = ((f32[8,1,171]{2,1,0:T(1,128)}), f32[8,1,171]{2,1,0:T(1,128)S(1)}, u32[]{:S(2)}, u32[]{:S(2)}) async-start(f32[8,1,171]{2,1,0:T(1,128)} %broadcast_in_dim.72), calls=%async_computation.1 | async-start | bytes 16384 | tf_op jit(solution)/shard_map/all_to_all | solution.py:24
  153.0 28.8 %copy-start.15 = (f32[57]{0:T(128)}, f32[57]{0:T(128)S(1)}, u32[]{:S(2)}) copy-start(f32[57]{0:T(128)S(1)} %get-tuple-element.394) | copy-start | bytes 688
  153.0 28.8 %copy-start.16 = (f32[57]{0:T(128)}, f32[57]{0:T(128)S(1)}, u32[]{:S(2)}) copy-start(f32[57]{0:T(128)S(1)} %get-tuple-element.395) | copy-start | bytes 688
  153.6 51.5 %copy-start.4 = (bf16[256,75]{0,1:T(8,128)(2,1)}, bf16[256,75]{0,1:T(8,128)(2,1)S(1)}, u32[]{:S(2)}) copy-start(bf16[256,75]{0,1:T(8,128)(2,1)S(1)} %multiply_convert_fusion.3) | copy-start | bytes 115204
  182.8 10.3 %all-to-all-start.1 = ((bf16[16,32,75]{2,1,0:T(8,128)(2,1)}), bf16[16,32,75]{2,1,0:T(8,128)(2,1)S(1)}, u32[]{:S(2)}, u32[]{:S(2)}) async-start(bf16[16,32,75]{2,1,0:T(8,128)(2,1)} %bitcast.8), calls=%async_computation.2 | async-start | bytes 262144 | tf_op jit(solution)/shard_map/all_to_all | solution.py:48
  186.9 89.9 %reduce-scatter.5.cloned.1.call-start = ((), (), s32[]{:S(2)}) async-start(), calls=%async_computation.10 | async-start | bytes 4456448 | tf_op jit(solution)/shard_map/reduce_scatter | solution.py:252
  187.0 6.0 %copy-start.11 = (f32[75]{0:T(128)}, f32[75]{0:T(128)S(1)}, u32[]{:S(2)}) copy-start(f32[75]{0:T(128)S(1)} %pad_maximum_fusion.1) | copy-start | bytes 904
  195.2 11.2 %copy-start.3 = (bf16[4096,256]{1,0:T(8,128)(2,1)S(1)}, bf16[4096,256]{1,0:T(8,128)(2,1)}, u32[]{:S(2)}) copy-start(bf16[4096,256]{1,0:T(8,128)(2,1)} %param.22) | copy-start | bytes 6291460
  209.7 67.1 %copy-start.1 = (bf16[32,4096]{1,0:T(8,128)(2,1)S(1)}, bf16[32,4096]{1,0:T(8,128)(2,1)}, u32[]{:S(2)}) copy-start(bf16[32,4096]{1,0:T(8,128)(2,1)} %reduce-scatter.3.cloned.1.call-done) | copy-start | bytes 786436
  282.4 56.8 %all-to-all-start.3 = ((bf16[16,32,4096]{2,1,0:T(8,128)(2,1)}), bf16[16,32,4096]{2,1,0:T(8,128)(2,1)}, u32[]{:S(2)}, u32[]{:S(2)}) async-start(bf16[16,32,4096]{2,1,0:T(8,128)(2,1)} %stack.2), calls=%async_computation.5 | async-start | bytes 8388608 | tf_op jit(solution)/shard_map/all_to_all | solution.py:18
  289.6 211.1 %all-reduce.8.cloned.1.call-start = ((), (), s32[]{:S(2)}) async-start(), calls=%async_computation.11 | async-start | bytes 12582912 | tf_op jit(solution)/shard_map/psum | solution.py:272
  353.5 10.1 %all-to-all-start.4 = ((f32[16,1,256]{2,1,0:T(1,128)}), f32[16,1,256]{2,1,0:T(1,128)S(1)}, u32[]{:S(2)}, u32[]{:S(2)}) async-start(f32[16,1,256]{2,1,0:T(1,128)} %bitcast.21), calls=%async_computation.6 | async-start | bytes 32768 | tf_op jit(solution)/shard_map/all_to_all | solution.py:65
  505.0 4.3 copy-start.2
Sparse Core Ops, SparseCore 0:
  9.6 48.6 all-gather.3
  66.0 68.0 reduce-scatter.2
  137.8 38.9 all-gather.5
  209.9 66.9 reduce-scatter.4
  353.6 147.0 all-reduce.7
